TPU v7x, 32 devices: a whole 2x2x4 slice. The times are simulated.
32 devices in a mesh: groups: 2 (over y), expert: 8 (over z, x), tensor: 2 (over core).
Axes of the slice: x: 2, y: 2, z: 4, core: 2. Of those that a mesh axis runs over, the one named last changes fastest.
Arguments:
- tokens: bfloat16 [1024, 1536], P(('groups', 'expert')), parts along dimension 0, may hold values from -12 to 12
- gain: float32 [1536], replicated, may hold values from 0.25 to 1.75
- route_ids: int32 [1024, 4], P(('groups', 'expert')), parts along dimension 0, may hold values from 0 to 3, as said below
- route_weights: float32 [1024, 4], P(('groups', 'expert')), parts along dimension 0, may hold values from 0.05 to 0.5
- w_gate: bfloat16 [8, 1536, 768], P('expert', None, 'tensor'), may hold values from -0.15625 to 0.15625
- w_up: bfloat16 [8, 1536, 768], P('expert', None, 'tensor'), may hold values from -0.15625 to 0.15625
- w_down: bfloat16 [8, 768, 1536], P('expert', 'tensor'), may hold values from -0.15625 to 0.15625
Outputs:
- mixed: bfloat16 [1024, 1536], P(('groups', 'expert')), parts along dimension 0
There are 2 independent parts, one for each index of `groups`. A program takes and returns all parts, laid end to end along the dimension named above; an argument that names none is the same for every part. Nothing has to cross between parts.
Inputs may be any that keep to these rules, and one draw needn't show every extreme that they name: `route_ids`: each row names 4 different experts. In each aligned block of 32 rows no expert is named more than 32 times; one expert, the same in every block, is named exactly 32 times in every block, and the other experts' counts within a block differ by at most one.
All inputs are finite; a program needn't handle non-finite values.
Results may differ from a plain program's by a relative error of at most 0.0045.
Values may be sent and summed in bfloat16 or wider, within the bound.
A program may use at most 64 MiB of HBM per device.

v0:
```python
import jax
import jax.numpy as jnp
from jax import lax
from jax.sharding import PartitionSpec as P


def gated_unit(gate_val, up_val):
    return gate_val * jax.nn.sigmoid(1.702 * gate_val) * (up_val + 1.0)


def route_tables(chosen_ids, chosen_weights, expert_count, slot_room):
    row_count, top_count = chosen_ids.shape
    matches = (chosen_ids[:, :, None] == jnp.arange(expert_count, dtype=jnp.int32)).astype(
        jnp.float32
    )
    flat_match = matches.reshape(row_count * top_count, expert_count)
    order_range = jnp.arange(row_count * top_count, dtype=jnp.int32)
    earlier = (order_range[:, None] > order_range[None, :]).astype(jnp.float32)
    before = jnp.dot(
        earlier, flat_match, precision=lax.Precision.HIGHEST, preferred_element_type=jnp.float32
    )
    position = jnp.sum(before * flat_match, axis=1).reshape(row_count, top_count).astype(jnp.int32)
    slot_index = chosen_ids * slot_room + position
    targets = jnp.arange(expert_count * slot_room, dtype=jnp.int32)
    slot_hits = slot_index[None, :, :] == targets[:, None, None]
    send_table = jnp.sum(slot_hits.astype(jnp.float32), axis=2).astype(jnp.bfloat16)
    mix_table = jnp.sum(jnp.where(slot_hits, chosen_weights[None, :, :], 0.0), axis=2)
    return (send_table, mix_table)


def per_device(tokens, gain, route_ids, route_weights, w_gate, w_up, w_down):
    expert_axis = lax.axis_size("expert")
    expert_count = expert_axis // 2
    tensor_count = lax.axis_size("tensor")
    own_rows = tokens.shape[0] // tensor_count
    top_count = route_ids.shape[1]
    capacity = max(2, own_rows * top_count // expert_count)
    gate_local = w_gate[0]
    up_local = w_up[0]
    down_local = w_down[0]
    first_row = lax.axis_index("tensor") * own_rows
    own_tokens = lax.dynamic_slice_in_dim(tokens, first_row, own_rows, 0)
    own_ids = lax.dynamic_slice_in_dim(route_ids, first_row, own_rows, 0)
    own_weights = lax.dynamic_slice_in_dim(route_weights, first_row, own_rows, 0)
    resident = own_tokens.astype(jnp.float32)
    inv_rms = lax.rsqrt(jnp.mean(resident * resident, axis=1, keepdims=True) + 1e-05)
    normed = (resident * inv_rms * gain).astype(jnp.bfloat16)
    send_table, mix_table = route_tables(own_ids, own_weights, expert_count, capacity)
    packed = jnp.dot(send_table, normed, preferred_element_type=jnp.float32).astype(jnp.bfloat16)
    features = packed.shape[1]
    by_expert = packed.reshape(expert_count, 1, capacity, features)
    outgoing = jnp.broadcast_to(by_expert, (expert_count, 2, capacity, features)).reshape(
        expert_axis * capacity, features
    )
    arrived = lax.all_to_all(outgoing, "expert", split_axis=0, concat_axis=0, tiled=True)
    row_piece = lax.all_gather(arrived, "tensor", axis=0, tiled=True)
    gate_val = jnp.dot(row_piece, gate_local, preferred_element_type=jnp.float32)
    up_val = jnp.dot(row_piece, up_local, preferred_element_type=jnp.float32)
    hidden = gated_unit(gate_val, up_val).astype(jnp.bfloat16)
    partial_value = lax.psum_scatter(
        jnp.dot(hidden, down_local, preferred_element_type=jnp.float32),
        "tensor",
        scatter_dimension=0,
        tiled=True,
    )
    returned = lax.all_to_all(
        partial_value.astype(jnp.bfloat16), "expert", split_axis=0, concat_axis=0, tiled=True
    ).astype(partial_value.dtype)
    expert_out = (
        returned.reshape(expert_count, 2, capacity, features)
        .sum(axis=1)
        .reshape(expert_count * capacity, features)
    )
    weighted = jnp.dot(
        mix_table.T, expert_out, precision=lax.Precision.HIGHEST, preferred_element_type=jnp.float32
    )
    finished = (resident + weighted).astype(jnp.bfloat16)
    return lax.all_gather(finished, "tensor", axis=0, tiled=True)


def solution(mesh):
    placed = (
        P(("groups", "expert"), None),
        P(),
        P(("groups", "expert"), None),
        P(("groups", "expert"), None),
        P("expert", None, "tensor"),
        P("expert", None, "tensor"),
        P("expert", "tensor", None),
    )
    return jax.shard_map(
        per_device,
        mesh=mesh,
        in_specs=placed,
        out_specs=P(("groups", "expert"), None),
        check_vma=False,
    )
```

profile of v0, /device:TPU:0, one launch (start us, length us, event | category | flops | bytes accessed | tf_op | source)
XLA Modules:
  0.0 106.2 jit_solution(7419597730249863763)
XLA Ops:
  6.5 0.0 copy-start
  6.5 0.0 all-gather.2.cloned.1.call-start
  6.5 1.1 %fusion.18 = f32[32]{0:T(128)S(1)} fusion(bf16[64,1536]{1,0:T(8,128)(2,1)} %param.7, s32[]{:T(128)S(6)} %select_n.9), kind=kLoop, calls=%fused_computation.24 | loop fusion | flops 147424 | bytes 98436 | tf_op jit(solution)/shard_map/reduce_sum | solution.py:46
  7.7 0.8 constant_dynamic-slice_fusion.1
  8.4 0.8 constant_dynamic-slice_fusion
  9.2 0.1 copy.14
  9.3 0.1 eq.30
  9.4 0.1 fusion.9
  9.5 0.1 convert_element_type.42
  9.7 0.1 copy.13
  9.7 0.1 convert_reduce_fusion.1
  9.9 1.2 %convolution_convert_fusion = bf16[128,1536]{1,0:T(8,128)(2,1)S(1)} fusion(f32[1536]{0:T(1024)} %param.8, f32[32]{0:T(128)S(1)} %add_rsqrt_fusion, bf16[64,1536]{1,0:T(8,128)(2,1)} %param.7, s32[]{:T(128)S(6)} %select_n.9, bf16[128,32]{0,1:T(8,128)(2,1)S(1)} %get-tuple-element.5), kind=kOutput, calls=%fused_computation | convolution fusion | flops 12976128 | bytes 508036 | tf_op jit(solution)/shard_map/dot_general | solution.py:49
  11.1 0.1 broadcast_in_dim.19
  11.2 27.3 %all_to_all.21 = bf16[8,32,1536]{2,1,0:T(8,128)(2,1)} all-to-all(bf16[8,32,1536]{2,1,0:T(8,128)(2,1)S(1)} %bitcast.25), channel_id=1, replica_groups=mesh['groups'=2,'expert'=8,'tensor'=2] {'expert'}, dimensions={0} | all-to-all | bytes 1572864 | tf_op jit(solution)/shard_map/all_to_all | solution.py:55
  38.5 0.0 all-gather.2.cloned.1.call-update
  38.5 0.0 reduce-scatter.2.cloned.1.call-start
  38.6 9.0 %all-gather.2.cloned.1.call-done = bf16[512,1536]{1,0:T(8,128)(2,1)} async-done(((bf16[256,1536]{1,0:T(8,128)(2,1)}), bf16[512,1536]{1,0:T(8,128)(2,1)}) %all-gather.2.cloned.1.call-update) | async-done | bytes 1572880 | tf_op jit(solution)/shard_map/all_gather | solution.py:56
  47.5 0.0 copy-start.2
  47.5 2.8 %fusion.7 = f32[512,384]{1,0:T(8,128)S(1)} fusion(bf16[512,1536]{1,0:T(8,128)(2,1)} %all-gather.2.cloned.1.call-done, bf16[1,1536,384]{2,1,0:T(8,128)(2,1)} %param.11), kind=kOutput, calls=%fused_computation.10 | convolution fusion | flops 603979776 | bytes 3538944 | tf_op jit(solution)/shard_map/dot_general | solution.py:57
  50.4 0.0 copy-done
  50.4 0.0 copy-done.2
  50.4 4.8 %fusion.3 = f32[512,1536]{1,0:T(8,128)} fusion(bf16[512,1536]{1,0:T(8,128)(2,1)S(1)} %copy-done.2, bf16[1,384,1536]{2,1,0:T(8,128)(2,1)S(1)} %copy-done, bf16[1,1536,384]{2,1,0:T(8,128)(2,1)} %param.12, f32[512,384]{1,0:T(8,128)S(1)} %fusion.7), kind=kOutput, calls=%fused_computation.7 | convolution fusion | flops 1209532416 | bytes 7864320 | tf_op jit(solution)/shard_map/dot_general | solution.py:61
  55.1 0.0 reduce-scatter.2.cloned.1.call-update
  55.2 12.5 %reduce-scatter.2.cloned.1.call-done = f32[256,1536]{1,0:T(8,128)} async-done(((f32[512,1536]{1,0:T(8,128)}), f32[256,1536]{1,0:T(8,128)}) %reduce-scatter.2.cloned.1.call-update) | async-done | bytes 1572880 | tf_op jit(solution)/shard_map/reduce_scatter | solution.py:60
  67.7 1.5 %convert_element_type.48 = bf16[256,1536]{1,0:T(8,128)(2,1)S(1)} convert(f32[256,1536]{1,0:T(8,128)} %reduce-scatter.2.cloned.1.call-done) | non-fusion elementwise | flops 393216 | bytes 2359296 | tf_op jit(solution)/shard_map/convert_element_type | solution.py:67
  69.1 26.1 %all_to_all.22 = bf16[8,32,1536]{2,1,0:T(8,128)(2,1)S(1)} all-to-all(bf16[8,32,1536]{2,1,0:T(8,128)(2,1)S(1)} %bitcast.26), channel_id=1, replica_groups=mesh['groups'=2,'expert'=8,'tensor'=2] {'expert'}, dimensions={0} | all-to-all | bytes 1572864 | tf_op jit(solution)/shard_map/all_to_all | solution.py:66
  95.3 0.0 copy-start.1
  95.3 0.1 convert_reduce_fusion
  95.4 0.8 copy-done.1
  96.2 0.5 fusion
  96.7 1.9 %all_gather.7 = bf16[64,1536]{1,0:T(8,128)(2,1)S(1)} all-gather(bf16[32,1536]{1,0:T(8,128)(2,1)S(1)} %fusion), channel_id=1, replica_groups=mesh['groups'=2,'expert'=8,'tensor'=2] {'tensor'}, dimensions={0}, use_global_device_ids=true | all-gather | bytes 294912 | tf_op jit(solution)/shard_map/all_gather | solution.py:78
  98.7 0.7 copy.16
  (3 shorter events, 0.0 us)
Async XLA Ops:
  6.5 43.8 %copy-start = (bf16[1,384,1536]{2,1,0:T(8,128)(2,1)S(1)}, bf16[1,384,1536]{2,1,0:T(8,128)(2,1)}, u32[]{:S(2)}) copy-start(bf16[1,384,1536]{2,1,0:T(8,128)(2,1)} %param.13) | copy-start | bytes 3538948
  6.5 41.0 %all-gather.2.cloned.1.call-start = ((), (), s32[]{:S(2)}) async-start(), calls=%async_computation.3 | async-start | bytes 2359296 | tf_op jit(solution)/shard_map/all_gather | solution.py:56
  38.5 29.1 %reduce-scatter.2.cloned.1.call-start = ((), (), s32[]{:S(2)}) async-start(), calls=%async_computation.4 | async-start | bytes 4718592 | tf_op jit(solution)/shard_map/reduce_scatter | solution.py:60
  47.5 2.9 %copy-start.2 = (bf16[512,1536]{1,0:T(8,128)(2,1)S(1)}, bf16[512,1536]{1,0:T(8,128)(2,1)}, u32[]{:S(2)}) copy-start(bf16[512,1536]{1,0:T(8,128)(2,1)} %all-gather.2.cloned.1.call-done) | copy-start | bytes 4718596
  95.3 0.9 copy-start.1
Sparse Core Ops, SparseCore 0:
  38.6 8.8 all-gather.1
  55.3 12.3 reduce-scatter.1
where the time goes:
time: 107 us; the launch traced here: 106 us
  blocking collectives  55.4 us (52%)
  waiting for transfers between devices  21.5 us (20%)
  between operations  13.5 us (13%)
  matrix products  9.5 us (9%)
  local copies, waits for them, and re-layouts  3.43 us (3%)
  other arithmetic  2.86 us (3%)
    all_to_all x1, blocking collectives, per_device(): lax.all_to_all(outgoing, 'expert', split_axis=0, concat_axis=0, tiled=True)  27.3 us
    all_to_all x1, blocking collectives, per_device(): lax.all_to_all(partial_value.astype(jnp.bfloat16), 'expert', split_axis=0...  26.1 us
    reduce_scatter x1, waiting for transfers between devices, per_device(): lax.psum_scatter(jnp.dot(hidden, down_local, preferred_element_type=jnp.f...  12.5 us
    all_gather x1, waiting for transfers between devices, per_device(): row_piece = lax.all_gather(arrived, 'tensor', axis=0, tiled=True)  8.95 us
    dot_general x1, matrix products, per_device(): jnp.dot(hidden, down_local, preferred_element_type=jnp.float32)  4.78 us
    dot_general x1, matrix products, per_device(): jnp.dot(row_piece, gate_local, preferred_element_type=jnp.float32)  2.83 us
  transfers between devices with their start and end apart: 2, of which 2 were waited for; matrix products, arithmetic and copies ran while one was open for 0% of the time, Pallas kernels for 0%

commit v1 on v0

--- a/solution.py
+++ b/solution.py
@@ -53,7 +53,9 @@
         expert_axis * capacity, features
     )
     arrived = lax.all_to_all(outgoing, "expert", split_axis=0, concat_axis=0, tiled=True)
-    row_piece = lax.all_gather(arrived, "tensor", axis=0, tiled=True)
+    row_piece = jnp.concatenate(
+        lax.all_to_all(jnp.stack([arrived] * lax.axis_size("tensor")), "tensor", 0, 0), axis=0
+    )
     gate_val = jnp.dot(row_piece, gate_local, preferred_element_type=jnp.float32)
     up_val = jnp.dot(row_piece, up_local, preferred_element_type=jnp.float32)
     hidden = gated_unit(gate_val, up_val).astype(jnp.bfloat16)

time: 107 us -> 98.1 us (0.917)
  waiting for transfers between devices: 21.5 us -> 10.4 us
  blocking collectives: 55.4 us -> 60.6 us
  matrix products: 9.5 us -> 7.65 us
    all_gather x1 -> x0, waiting for transfers between devices: 8.95 us -> none  [per_device(): row_piece = lax.all_gather(arrived, 'tensor', axis=0, tiled=True)]
    all_to_all x0 -> x1, blocking collectives: none -> 5.13 us  [per_device(): lax.all_to_all(jnp.stack([arrived] * lax.axis_size('tensor')), 'tensor',...]
    reduce_scatter x1, waiting for transfers between devices: 12.5 us -> 10.4 us  [per_device(): lax.psum_scatter(jnp.dot(hidden, down_local, preferred_element_type=jnp.f...]
    dot_general x1, matrix products: 2.83 us -> 0.97 us  [per_device(): jnp.dot(row_piece, gate_local, preferred_element_type=jnp.float32)]
  transfers between devices with their start and end apart: 2 -> 1, of which waited for: 2 -> 1; matrix products, arithmetic and copies ran while one was open for 0% -> 0% of each run, Pallas kernels for 0% -> 0%
where the time goes in v1:
time: 98.1 us; the launch traced here: 97.7 us
  blocking collectives  60.6 us (62%)
  between operations  13.5 us (14%)
  waiting for transfers between devices  10.4 us (11%)
  matrix products  7.65 us (8%)
  other arithmetic  3 us (3%)
  local copies, waits for them, and re-layouts  2.64 us (3%)
    all_to_all x1, blocking collectives, per_device(): lax.all_to_all(outgoing, 'expert', split_axis=0, concat_axis=0, tiled=True)  27.2 us
    all_to_all x1, blocking collectives, per_device(): lax.all_to_all(partial_value.astype(jnp.bfloat16), 'expert', split_axis=0...  26.3 us
    reduce_scatter x1, waiting for transfers between devices, per_device(): lax.psum_scatter(jnp.dot(hidden, down_local, preferred_element_type=jnp.f...  10.4 us
    all_to_all x1, blocking collectives, per_device(): lax.all_to_all(jnp.stack([arrived] * lax.axis_size('tensor')), 'tensor',...  5.13 us
    dot_general x1, matrix products, per_device(): jnp.dot(hidden, down_local, preferred_element_type=jnp.float32)  4.77 us
  transfers between devices with their start and end apart: 1, of which 1 were waited for; matrix products, arithmetic and copies ran while one was open for 0% of the time, Pallas kernels for 0%

profile of v1, /device:TPU:0, one launch (start us, length us, event | category | flops | bytes accessed | tf_op | source)
XLA Modules:
  0.0 97.7 jit_solution(5081696575463794640)
XLA Ops:
  6.5 0.0 copy-start
  6.5 0.0 reduce-scatter.2.cloned.1.call-start
  6.5 1.1 %fusion.18 = f32[32]{0:T(128)S(1)} fusion(bf16[64,1536]{1,0:T(8,128)(2,1)} %param.7, s32[]{:T(128)S(6)} %select_n.9), kind=kLoop, calls=%fused_computation.25 | loop fusion | flops 147424 | bytes 98436 | tf_op jit(solution)/shard_map/reduce_sum | solution.py:46
  7.7 0.8 constant_dynamic-slice_fusion.1
  8.4 0.8 constant_dynamic-slice_fusion
  9.2 0.1 copy.14
  9.3 0.1 eq.30
  9.4 0.1 fusion.9
  9.5 0.1 convert_element_type.42
  9.7 0.1 copy.13
  9.7 0.1 convert_reduce_fusion.1
  9.9 1.2 %convolution_convert_fusion = bf16[128,1536]{1,0:T(8,128)(2,1)S(1)} fusion(f32[1536]{0:T(1024)} %param.8, f32[32]{0:T(128)S(1)} %add_rsqrt_fusion, bf16[64,1536]{1,0:T(8,128)(2,1)} %param.7, s32[]{:T(128)S(6)} %select_n.9, bf16[128,32]{0,1:T(8,128)(2,1)S(1)} %get-tuple-element.5), kind=kOutput, calls=%fused_computation | convolution fusion | flops 12976128 | bytes 508036 | tf_op jit(solution)/shard_map/dot_general | solution.py:49
  11.1 0.1 broadcast_in_dim.19
  11.2 27.2 %all_to_all.23 = bf16[8,32,1536]{2,1,0:T(8,128)(2,1)S(1)} all-to-all(bf16[8,32,1536]{2,1,0:T(8,128)(2,1)S(1)} %bitcast.25), channel_id=1, replica_groups=mesh['groups'=2,'expert'=8,'tensor'=2] {'expert'}, dimensions={0} | all-to-all | bytes 1572864 | tf_op jit(solution)/shard_map/all_to_all | solution.py:55
  38.4 0.1 pad_maximum_fusion
  38.5 0.0 copy-start.2
  38.5 5.1 %all_to_all.24 = bf16[2,256,1536]{2,1,0:T(8,128)(2,1)S(1)} all-to-all(bf16[2,256,1536]{2,1,0:T(8,128)(2,1)S(1)} %pad_maximum_fusion), channel_id=1, replica_groups=mesh['groups'=2,'expert'=8,'tensor'=2] {'tensor'}, dimensions={0} | all-to-all | bytes 3145728 | tf_op jit(solution)/shard_map/all_to_all | solution.py:57
  43.7 0.0 copy-done.2
  43.7 1.0 fusion.7
  44.6 0.0 copy-done
  44.7 4.8 %fusion.3 = f32[512,1536]{1,0:T(8,128)} fusion(bf16[512,1536]{1,0:T(8,128)(2,1)S(1)} %bitcast.29, bf16[1,384,1536]{2,1,0:T(8,128)(2,1)S(1)} %copy-done, bf16[1,1536,384]{2,1,0:T(8,128)(2,1)} %param.12, f32[512,384]{1,0:T(8,128)S(1)} %fusion.7), kind=kOutput, calls=%fused_computation.8 | convolution fusion | flops 1209532416 | bytes 7864320 | tf_op jit(solution)/shard_map/dot_general | solution.py:63
  49.4 0.0 reduce-scatter.2.cloned.1.call-update
  49.5 10.4 %reduce-scatter.2.cloned.1.call-done = f32[256,1536]{1,0:T(8,128)} async-done(((f32[512,1536]{1,0:T(8,128)}), f32[256,1536]{1,0:T(8,128)}) %reduce-scatter.2.cloned.1.call-update) | async-done | bytes 1572880 | tf_op jit(solution)/shard_map/reduce_scatter | solution.py:62
  59.8 1.5 %convert_element_type.48 = bf16[256,1536]{1,0:T(8,128)(2,1)S(1)} convert(f32[256,1536]{1,0:T(8,128)} %reduce-scatter.2.cloned.1.call-done) | non-fusion elementwise | flops 393216 | bytes 2359296 | tf_op jit(solution)/shard_map/convert_element_type | solution.py:69
  61.3 0.0 copy-start.1
  61.3 26.3 %all_to_all.25 = bf16[8,32,1536]{2,1,0:T(8,128)(2,1)S(1)} all-to-all(bf16[8,32,1536]{2,1,0:T(8,128)(2,1)S(1)} %bitcast.27), channel_id=1, replica_groups=mesh['groups'=2,'expert'=8,'tensor'=2] {'expert'}, dimensions={0} | all-to-all | bytes 1572864 | tf_op jit(solution)/shard_map/all_to_all | solution.py:68
  87.6 0.1 convert_reduce_fusion
  87.7 0.0 copy-done.1
  87.7 0.5 fusion
  88.2 1.9 %all_gather.3 = bf16[64,1536]{1,0:T(8,128)(2,1)S(1)} all-gather(bf16[32,1536]{1,0:T(8,128)(2,1)S(1)} %fusion), channel_id=1, replica_groups=mesh['groups'=2,'expert'=8,'tensor'=2] {'tensor'}, dimensions={0}, use_global_device_ids=true | all-gather | bytes 294912 | tf_op jit(solution)/shard_map/all_gather | solution.py:80
  90.2 0.7 copy.16
  (3 shorter events, 0.0 us)
Async XLA Ops:
  6.5 38.1 %copy-start = (bf16[1,384,1536]{2,1,0:T(8,128)(2,1)S(1)}, bf16[1,384,1536]{2,1,0:T(8,128)(2,1)}, u32[]{:S(2)}) copy-start(bf16[1,384,1536]{2,1,0:T(8,128)(2,1)} %param.13) | copy-start | bytes 3538948
  6.5 53.3 %reduce-scatter.2.cloned.1.call-start = ((), (), s32[]{:S(2)}) async-start(), calls=%async_computation.4 | async-start | bytes 4718592 | tf_op jit(solution)/shard_map/reduce_scatter | solution.py:62
  38.5 5.1 %copy-start.2 = (bf16[1,1536,384]{2,1,0:T(8,128)(2,1)S(1)}, bf16[1,1536,384]{2,1,0:T(8,128)(2,1)}, u32[]{:S(2)}) copy-start(bf16[1,1536,384]{2,1,0:T(8,128)(2,1)} %param.11) | copy-start | bytes 3538948
  61.3 26.4 %copy-start.1 = (bf16[64,1536]{1,0:T(8,128)(2,1)S(1)}, bf16[64,1536]{1,0:T(8,128)(2,1)}, u32[]{:S(2)}) copy-start(bf16[64,1536]{1,0:T(8,128)(2,1)} %param.7) | copy-start | bytes 589828
Sparse Core Ops, SparseCore 0:
  49.6 10.1 reduce-scatter.1
